TPU v7x, 32 devices: a whole 2x2x4 slice. The times are simulated.
32 devices in a mesh: seq: 16 (over z, y, x), head: 2 (over core).
Axes of the slice: x: 2, y: 2, z: 4, core: 2. Of those that a mesh axis runs over, the one named last changes fastest.
Arguments:
- queries: bfloat16 [4096, 64, 192], P('seq', 'head'), may hold values from -50 to 50
- grad_out: bfloat16 [4096, 64, 128], P('seq', 'head'), may hold values from -6 to 6
- latent: bfloat16 [4096, 576], P('seq'), may hold values from -18 to 18
- w_uk: bfloat16 [64, 512, 128], P('head'), may hold values from -0.25 to 0.25
- w_uv: bfloat16 [64, 512, 128], P('head'), may hold values from -0.25 to 0.25
- doc_start: int32 [4096], P('seq'), may hold values from 0 to 4095, as said below
Outputs:
- grad_query: bfloat16 [4096, 64, 192], P('seq', 'head')
- grad_latent: float32 [4096, 576], P(('seq', 'head'))
Inputs may be any that keep to these rules, and one draw needn't show every extreme that they name: doc_start[t] is the first position of the document that holds position t; documents follow one another, each of 1 to 768 positions, and one is exactly 768 long.
All inputs are finite; a program needn't handle non-finite values.
Results may differ from a plain program's by a relative error of at most 0.008.
Values may be sent and summed in bfloat16 or wider, within the bound.
A program may use at most 192 MiB of HBM per device.

v0:
```python
import functools
import math

import jax
import jax.numpy as jnp
from jax import lax
from jax.experimental import pallas as pl
from jax.experimental.pallas import tpu as pltpu
from jax.sharding import PartitionSpec as P

BACK = 3
LANES = 128
PAIR = 2
GROUP = 2
HIDDEN = -1e30
F32 = jnp.float32
BF16 = jnp.bfloat16
NN = (((1,), (0,)), ((), ()))
NT = (((1,), (1,)), ((), ()))


def dot(a, b, dims=NN):
    return lax.dot_general(a, b, dims, preferred_element_type=F32)


def kernel(tokens, nope, latw, factor, halves, counts, side, starts, q_ref, g_ref, uk_ref, uv_ref, kt_ref,
           gq_ref, *refs):
    *sums, k_ref, bias_ref, acc_ref, qc_ref, gl_ref, dqa_ref = refs
    step = pl.program_id(0)
    width, span = kt_ref.shape
    blocks = tokens // LANES

    @pl.when(step == 0)
    def _():
        acc_ref[...] = jnp.zeros_like(acc_ref)
        for j in range(span // LANES):
            part = pl.ds(j * LANES, LANES)
            k_ref[part, :] = kt_ref[:, part].T
            kpos = lax.broadcasted_iota(jnp.int32, (LANES, tokens), 0) + j * LANES
            qpos = lax.broadcasted_iota(jnp.int32, (LANES, tokens), 1) + (span - tokens)
            seen = (kpos >= starts[...]) & (kpos <= qpos)
            bias_ref[part, :] = jnp.where(seen, 0.0, HIDDEN)

    def pair(index, carry):
        first = index * PAIR
        for i in range(PAIR):
            columns = pl.ds(i * LANES, LANES)
            q_abs = dot(uk_ref[first + i], q_ref[first + i, :nope, :]).astype(BF16)
            grad_lat = dot(uv_ref[first + i], g_ref[first + i], NT).astype(BF16)
            for b in range(blocks):
                here = slice(b * LANES, (b + 1) * LANES)
                qc_ref[b, :latw, columns] = q_abs[:, here]
                qc_ref[b, latw:, columns] = q_ref[first + i, nope:, here]
                gl_ref[b, :, columns] = grad_lat[:, here]

        def attend(b, count):
            end = span - (blocks - 1 - b) * LANES
            rows = slice(end - count * LANES, end)
            here = slice(b * LANES, (b + 1) * LANES)
            bias = bias_ref[rows, here]
            scores = dot(k_ref[rows, :], qc_ref[b]) + jnp.concatenate([bias] * PAIR, 1)
            dprob = dot(k_ref[rows, :latw], gl_ref[b])
            top = jnp.max(scores, 0, keepdims=True)
            expo = jnp.exp2((scores - top) * (factor * math.log2(math.e)))
            probs = (expo * (1.0 / jnp.sum(expo, 0, keepdims=True))).astype(BF16)
            wide = probs.astype(F32)
            delta = jnp.sum(wide * dprob, 0, keepdims=True)
            dscore = (wide * (dprob - delta)).astype(BF16)
            dvalue = dot(gl_ref[b], probs, NT) * (1.0 / factor)
            dq = dot(kt_ref[:, rows], dscore) * factor
            dkey = dot(qc_ref[b], dscore, NT)
            acc_ref[:latw, rows] += dkey[:latw] + dvalue
            acc_ref[latw:, rows] += dkey[latw:]
            for i in range(PAIR):
                columns = slice(i * LANES, (i + 1) * LANES)
                dqa_ref[i, :, here] = dq[:latw, columns].astype(BF16)
                gq_ref[first + i, nope:, here] = dq[latw:, columns].astype(BF16)

        most = span // LANES - blocks + 1
        sizes = sorted({2, 4, *range(5, most), most})
        for b in range(blocks):
            least = 0
            for size in sizes:
                count = counts[b]
                fits = (count > least) & (count <= size)
                pl.when(fits)(functools.partial(attend, b, size))
                least = size

        for i in range(PAIR):
            gq_ref[first + i, :nope, :] = dot(uk_ref[first + i].T, dqa_ref[i]).astype(BF16)
        return carry

    lax.fori_loop(0, q_ref.shape[0] // PAIR, pair, 0)

    @pl.when(step == pl.num_programs(0) - 1)
    def _():
        if not halves:
            for r in range(span // tokens):
                sums[0][r] = acc_ref[:, r * tokens:(r + 1) * tokens] * factor
            return
        mine_ref, theirs_ref = sums
        half = tokens // 2
        for r in range(span // tokens):
            own = pl.ds(pl.multiple_of(r * tokens + side[0] * half, half), half)
            other = pl.ds(pl.multiple_of(r * tokens + (1 - side[0]) * half, half), half)
            mine_ref[r] = acc_ref[:, own] * factor
            theirs_ref[r] = (acc_ref[:, other] * factor).astype(BF16)


def places():
    me = lax.axis_index("seq")
    count = lax.axis_size("seq")
    head = lax.axis_index("head")
    ahead = [(lax.rem(me + r, count), head) for r in range(1, BACK + 1)]
    behind = [(lax.rem(me + count - r, count), head) for r in range(1, BACK + 1)]
    return head, ahead, behind, (me, 1 - head)


def meet(peers):
    barrier = pltpu.get_barrier_semaphore()
    for peer in peers:
        pl.semaphore_signal(barrier, inc=1, device_id=peer, device_id_type=pl.DeviceIdType.MESH)
    pl.semaphore_wait(barrier, len(peers))


def send(src, dst, sems, slot, peer):
    copy = pltpu.make_async_remote_copy(
        src_ref=src, dst_ref=dst, send_sem=sems.at[0, slot], recv_sem=sems.at[1, slot],
        device_id=peer, device_id_type=pl.DeviceIdType.MESH,
    )
    copy.start()
    return copy


def gather_kernel(own_ref, keys_ref, far_sems, near_sems):
    tokens = own_ref.shape[1]
    half = tokens // 2
    head, ahead, behind, sibling = places()
    meet(ahead + behind + [sibling])
    mine = pl.ds(pl.multiple_of(head * half, half), half)
    landing = [
        keys_ref.at[:, pl.ds(pl.multiple_of((BACK - r) * tokens + head * half, half), half)]
        for r in range(1, BACK + 1)
    ]
    far = [send(own_ref.at[:, mine], landing[r], far_sems, r, ahead[r]) for r in range(BACK)]
    keys_ref[:, BACK * tokens:] = own_ref[...]
    near = []
    for r in range(BACK):
        far[r].wait_recv()
        near.append(send(landing[r], landing[r], near_sems, r, sibling))
    for r in range(BACK):
        far[r].wait_send()
        near[r].wait()


def gather(own):
    width, tokens = own.shape
    return pl.pallas_call(
        gather_kernel,
        out_shape=jax.ShapeDtypeStruct((width, (BACK + 1) * tokens), own.dtype),
        in_specs=[pl.BlockSpec(memory_space=pltpu.VMEM)],
        out_specs=pl.BlockSpec(memory_space=pltpu.VMEM),
        scratch_shapes=[pltpu.SemaphoreType.DMA((2, BACK)), pltpu.SemaphoreType.DMA((2, BACK))],
        compiler_params=pltpu.CompilerParams(collective_id=0, has_side_effects=True),
        name="gather",
    )(own)


def combine_kernel(mine_ref, theirs_ref, out_ref, near_ref, part_ref, far_ref, near_sems, far_sems):
    _, ahead, behind, sibling = places()
    meet(ahead + behind + [sibling])
    near = [
        send(theirs_ref.at[r], near_ref.at[r], near_sems, r, sibling) for r in range(BACK + 1)
    ]
    far = []
    for r in range(BACK):
        near[r].wait_recv()
        part_ref[r] = (mine_ref[r] + near_ref[r].astype(F32)).astype(BF16)
        far.append(send(part_ref.at[r], far_ref.at[r], far_sems, r, behind[BACK - 1 - r]))
    near[BACK].wait_recv()
    out_ref[...] = mine_ref[BACK] + near_ref[BACK].astype(F32)
    for r in range(BACK):
        far[r].wait_recv()
        out_ref[...] += far_ref[r].astype(F32)
    for r in range(BACK + 1):
        near[r].wait_send()
    for r in range(BACK):
        far[r].wait_send()


def combine(mine, theirs):
    shape = mine.shape[1:]
    return pl.pallas_call(
        combine_kernel,
        out_shape=jax.ShapeDtypeStruct(shape, F32),
        in_specs=[pl.BlockSpec(memory_space=pltpu.VMEM)] * 2,
        out_specs=pl.BlockSpec(memory_space=pltpu.VMEM),
        scratch_shapes=[
            pltpu.VMEM((BACK + 1,) + shape, BF16),
            pltpu.VMEM((BACK,) + shape, BF16),
            pltpu.VMEM((BACK,) + shape, BF16),
            pltpu.SemaphoreType.DMA((2, BACK + 1)),
            pltpu.SemaphoreType.DMA((2, BACK)),
        ],
        compiler_params=pltpu.CompilerParams(collective_id=1, has_side_effects=True),
        name="combine",
    )(mine, theirs)


def shift(block, axis, distance):
    devices = range(lax.axis_size(axis))
    route = [(i - distance, i) for i in devices if i - distance in devices]
    return lax.ppermute(block, axis, route)


def shards(queries, grad_out, latent, w_uk, w_uv, doc_start):
    tokens, heads, depth = queries.shape
    width = latent.shape[1]
    latw, nope = w_uk.shape[1:]
    vdim = w_uv.shape[2]
    span = (BACK + 1) * tokens
    blocks = tokens // LANES
    factor = depth ** (-0.5)
    own = latent.T
    halves = lax.axis_size("head") == 2
    if halves:
        keys = gather(own)
    else:
        received = [shift(own, "seq", level) for level in range(BACK, 0, -1)]
        keys = jnp.concatenate(received + [own], 1)
    starts = doc_start - (lax.axis_index("seq") - BACK) * tokens
    ends = (span - tokens) // LANES + 1 + jnp.arange(blocks, dtype=jnp.int32)
    counts = ends - starts[::LANES] // LANES
    side = lax.axis_index("head").astype(jnp.int32)[None]
    share = tokens // 2 if halves else tokens
    sums = [F32, BF16] if halves else [F32]

    def per_pair(*shape):
        return pl.BlockSpec((PAIR * GROUP,) + shape, lambda p, *_: (p, 0, 0))

    def whole(*shape):
        return pl.BlockSpec(shape, lambda p, *_: (0,) * len(shape))

    grad_q, mine, *theirs = pl.pallas_call(
        functools.partial(kernel, tokens, nope, latw, factor, halves),
        grid_spec=pltpu.PrefetchScalarGridSpec(
            num_scalar_prefetch=2,
            grid=(heads // (PAIR * GROUP),),
            in_specs=[
                whole(1, tokens),
                per_pair(depth, tokens),
                per_pair(tokens, vdim),
                per_pair(latw, nope),
                per_pair(latw, vdim),
                whole(width, span),
            ],
            out_specs=[
                per_pair(depth, tokens),
                *[whole(BACK + 1, width, share) for _ in sums],
            ],
            scratch_shapes=[
                pltpu.VMEM((span, width), BF16),
                pltpu.VMEM((span, tokens), F32),
                pltpu.VMEM((width, span), F32),
                pltpu.VMEM((blocks, width, PAIR * LANES), BF16),
                pltpu.VMEM((blocks, latw, PAIR * LANES), BF16),
                pltpu.VMEM((PAIR, latw, tokens), BF16),
            ],
        ),
        out_shape=[
            jax.ShapeDtypeStruct((heads, depth, tokens), BF16),
            *[jax.ShapeDtypeStruct((BACK + 1, width, share), kind) for kind in sums],
        ],
        compiler_params=pltpu.CompilerParams(
            dimension_semantics=("arbitrary",), vmem_limit_bytes=60 * 1024 * 1024
        ),
        name="attend",
    )(
        counts,
        side,
        starts[None, :],
        queries.transpose(1, 2, 0),
        grad_out.transpose(1, 0, 2),
        w_uk,
        w_uv,
        keys,
    )
    grad_query = grad_q.transpose(2, 0, 1)
    if halves:
        return grad_query, combine(mine, theirs[0]).T
    back = [shift(mine[BACK - r].astype(BF16), "seq", -r) for r in range(1, BACK + 1)]
    total = mine[BACK]
    for piece in back:
        total = total + piece.astype(F32)
    return grad_query, lax.psum_scatter(total.T, "head", scatter_dimension=0, tiled=True)


def solution(mesh):
    placed = (
        P("seq", "head", None),
        P("seq", "head", None),
        P("seq", None),
        P("head", None, None),
        P("head", None, None),
        P("seq"),
    )
    return jax.shard_map(
        shards,
        mesh=mesh,
        in_specs=placed,
        out_specs=(P("seq", "head", None), P(("seq", "head"), None)),
        check_vma=False,
    )
```

profile of v0, /device:TPU:0, one launch (start us, length us, event | category | flops | bytes accessed | tf_op | source)
XLA Modules:
  0.0 127.3 jit_solution(12375842865638119405)
XLA Ops:
  0.6 0.7 broadcast_subtract_fusion
  1.3 0.0 copy-start
  1.3 0.1 slice.3
  1.4 0.6 fusion.counts
  2.0 17.8 %gather.1.kt_ref = bf16[576,1024]{1,0:T(8,128)(2,1)} custom-call(bf16[576,256]{1,0:T(8,128)(2,1)} %bitcast.12), custom_call_target="tpu_custom_call" | custom-call | tf_op jit(solution)/shard_map/gather/pallas_call | solution.py:158
  19.8 3.7 %copy.10 = bf16[256,32,128]{2,0,1:T(8,128)(2,1)} copy(bf16[256,32,128]{2,1,0:T(8,128)(2,1)} %param.7) | data formatting | bytes 4194304 | tf_op args[1]
  23.5 0.0 copy-done
  23.5 46.7 %attend.1 = (bf16[32,192,256]{2,1,0:T(8,128)(2,1)}, f32[4,576,128]{2,1,0:T(8,128)}, bf16[4,576,128]{2,1,0:T(8,128)(2,1)}) custom-call(s32[2]{0:T(128)} %fusion.counts, s32[1]{0:T(128)} %bitcast.side, s32[1,256]{1,0:T(1,128)} %bitcast.13, bf16[32,192,256]{2,1,0:T(8,128)(2,1)} %bitcast.10, bf16[32,256,128]{2,1,0:T(8,128)(2,1)} %bitcast.9, ...), custom_call_target="tpu_custom_call" | custom-call | tf_op jit(solution)/shard_map/attend/pallas_call | solution.py:244
  70.2 55.3 %combine.1 = f32[576,128]{1,0:T(8,128)} custom-call(f32[4,576,128]{2,1,0:T(8,128)} %get-tuple-element.6.mine_ref, bf16[4,576,128]{2,1,0:T(8,128)(2,1)} %get-tuple-element.7.theirs_ref), custom_call_target="tpu_custom_call" | custom-call | tf_op jit(solution)/shard_map/combine/pallas_call | solution.py:193
  125.6 1.7 %copy.12 = f32[128,576]{0,1:T(8,128)} copy(f32[128,576]{0,1:T(8,128)} %bitcast.11) | data formatting | bytes 589824
Async XLA Ops:
  1.3 22.2 %copy-start = (s32[256]{0:T(256)}, s32[256]{0:T(256)S(1)}, u32[]{:S(2)}) copy-start(s32[256]{0:T(256)S(1)} %broadcast_subtract_fusion) | copy-start | bytes 3076
where the time goes:
time: 125 us; the launch traced here: 127 us
  Pallas kernels  120 us (96%)
  local copies, waits for them, and re-layouts  5.54 us (4%)
  other arithmetic  1.26 us (1%)
    pallas_call x1, Pallas kernels, combine(): pl.pallas_call(combine_kernel, out_shape=jax.ShapeDtypeStruct(shape, F32)...  55.3 us
    pallas_call x1, Pallas kernels, shards(): pl.pallas_call(functools.partial(kernel, tokens, nope, latw, factor, halv...  46.7 us
    pallas_call x1, Pallas kernels, gather(): pl.pallas_call(gather_kernel, out_shape=jax.ShapeDtypeStruct((width, (BAC...  17.8 us
    unnamed x4, local copies, waits for them, and re-layouts  5.44 us

commit v1 on v0

v1 whole, which is shorter than its diff:
```python
import functools
import math

import jax
import jax.numpy as jnp
from jax import lax
from jax.experimental import pallas as pl
from jax.experimental.pallas import tpu as pltpu
from jax.sharding import PartitionSpec as P

BACK = 3
LANES = 128
STRIP = 32
HIDDEN = -1e30
F32 = jnp.float32
BF16 = jnp.bfloat16
NN = (((1,), (0,)), ((), ()))
NT = (((1,), (1,)), ((), ()))


def dot(a, b, dims=NN):
    return lax.dot_general(a, b, dims, preferred_element_type=F32)


def attend_kernel(tokens, factor, halves, sizes, count, side, starts, q_hbm, g_hbm, uk_hbm, uv_hbm, kt_ref,
                  gq_hbm, *refs):
    sums = refs[:2] if halves else refs[:1]
    (q_ref, g_ref, uk_ref, uv_ref, gq_ref, lat_ref, bias_ref, acc_ref, kv_ref, score_refs, dprob_refs,
     probs_refs, dscore_refs, dkv_refs, top_refs, inverse_refs, in_sems, out_sems) = refs[len(sums):]
    width, span = kt_ref.shape
    heads, depth, _ = q_ref.shape
    latw, nope = uk_ref.shape[1:]
    sources = [(q_hbm, q_ref), (g_hbm, g_ref), (uk_hbm, uk_ref), (uv_hbm, uv_ref)]

    def fetch(index, which):
        source, target = sources[which]
        return pltpu.make_async_copy(source.at[index], target.at[index], in_sems.at[which, index])

    def put(index):
        return pltpu.make_async_copy(gq_ref.at[index], gq_hbm.at[index], out_sems.at[index])

    def start(index, carry):
        for which in range(len(sources)):
            fetch(index, which).start()
        return carry

    lax.fori_loop(0, heads, start, 0)
    acc_ref[...] = jnp.zeros_like(acc_ref)
    for j in range(span // LANES):
        part = pl.ds(j * LANES, LANES)
        lat_ref[part, :] = kt_ref[:, part].T
        kpos = lax.broadcasted_iota(jnp.int32, (LANES, tokens), 0) + j * LANES
        qpos = lax.broadcasted_iota(jnp.int32, (LANES, tokens), 1) + (span - tokens)
        seen = (kpos >= starts[...]) & (kpos <= qpos)
        bias_ref[part, :] = jnp.where(seen, 0.0, HIDDEN)
    for slot in range(2):
        for ref in (score_refs, dprob_refs, probs_refs, dscore_refs, top_refs, inverse_refs):
            ref[slot][...] = jnp.zeros_like(ref[slot])
    kv_ref[...] = jnp.zeros_like(kv_ref)

    def run(size):
        rows = slice(span - size, span)
        chunks = [slice(r, r + STRIP) for r in range(span - size, span, STRIP)]
        trips = heads // 2 + 1

        def both(index):
            return jnp.concatenate([uk_ref[index], uv_ref[index]], 1)

        def half(trip, slot):
            turn = trip * 2 + slot
            first = jnp.minimum(turn, heads - 1)
            last = jnp.clip(turn - 2, 0, heads - 1)
            now, before = lax.rem(turn, 4), lax.rem(turn + 2, 4)
            probs, dscore = probs_refs[slot], dscore_refs[slot]
            inverse = inverse_refs[slot][...]
            kv = dot(lat_ref[rows, :latw], both(first)).astype(BF16)
            kv_ref[now, rows, :] = kv
            turned = (g_ref[last].T.astype(F32) * inverse).astype(BF16)
            dvalue = dot(probs[rows, :], turned, NT)
            query = (q_ref[last].astype(F32) * (inverse * factor)).astype(BF16)
            dkey = dot(dscore[rows, :], query, NT)
            key = jnp.concatenate([kv[:, :nope], lat_ref[rows, latw:]], 1)
            scores = dot(key, q_ref[first]) + bias_ref[rows, :]
            score_refs[slot][rows, :] = scores
            top_refs[slot][...] = jnp.max(scores, 0, keepdims=True)
            dkv_refs[slot][rows, :nope] = dkey[:, :nope].astype(BF16)
            dkv_refs[slot][rows, nope:] = dvalue.astype(BF16)
            acc_ref[rows, latw:] += dkey[:, nope:]
            if slot:
                pair = jnp.concatenate([dkv_refs[0][rows, :], dkv_refs[1][rows, :]], 1)
                other = jnp.maximum(last - 1, 0)
                weights = jnp.concatenate([both(other), both(last)], 1)
                acc_ref[rows, :latw] += dot(pair, weights, NT)
            dprob_refs[slot][rows, :] = dot(kv[:, nope:], g_ref[first], NT)
            key = jnp.concatenate([kv_ref[before, rows, :nope], lat_ref[rows, latw:]], 1)
            dq = dot(key.T, dscore[rows, :])
            gq_ref[last] = (dq * (inverse * factor)).astype(BF16)

        def normalize(slot, turn):
            score_ref, dprob_ref = score_refs[slot], dprob_refs[slot]
            probs_ref, dscore_ref = probs_refs[slot], dscore_refs[slot]
            top = top_refs[slot][...]
            total = jnp.zeros((STRIP, tokens), F32)
            delta = jnp.zeros((STRIP, tokens), F32)
            for part in chunks:
                expo = jnp.exp2((score_ref[part, :] - top) * (factor * math.log2(math.e)))
                probs_ref[part, :] = expo.astype(BF16)
                total += expo
                delta += expo * dprob_ref[part, :]
            inverse = 1.0 / jnp.sum(total, 0, keepdims=True)
            delta = jnp.sum(delta, 0, keepdims=True) * inverse
            valid = jnp.where((turn >= 0) & (turn < heads), 1.0, 0.0)
            inverse_refs[slot][...] = inverse * valid
            for part in chunks:
                expo = probs_ref[part, :].astype(F32)
                dscore_ref[part, :] = (expo * (dprob_ref[part, :] - delta)).astype(BF16)

        def step(trip, carry):
            @pl.when(trip < trips - 1)
            def _():
                for which in range(len(sources)):
                    fetch(trip * 2, which).wait()
                    fetch(trip * 2 + 1, which).wait()

            half(trip, 0)
            normalize(1, trip * 2 - 1)
            half(trip, 1)
            normalize(0, trip * 2)

            @pl.when(trip > 0)
            def _():
                put(trip * 2 - 2).start()
                put(trip * 2 - 1).start()

            return carry

        lax.fori_loop(0, trips, step, 0)

    least = 0
    for size in sizes:
        pl.when((count[0] * LANES > least) & (count[0] * LANES <= size))(functools.partial(run, size))
        least = size

    if halves:
        mine_ref, theirs_ref = sums
        half = tokens // 2
        for r in range(span // tokens):
            own = pl.ds(pl.multiple_of(r * tokens + side[0] * half, half), half)
            other = pl.ds(pl.multiple_of(r * tokens + (1 - side[0]) * half, half), half)
            mine_ref[r] = acc_ref[own, :].T
            theirs_ref[r] = acc_ref[other, :].astype(BF16).T
    else:
        for r in range(span // tokens):
            sums[0][r] = acc_ref[r * tokens:(r + 1) * tokens, :].T

    def finish(index, carry):
        put(index).wait()
        return carry

    lax.fori_loop(0, heads, finish, 0)


def attend(count, side, starts, q, g, uk, uv, keys, halves):
    heads, depth, tokens = q.shape
    latw, nope = uk.shape[1:]
    vdim = uv.shape[2]
    width, span = keys.shape
    share = tokens // 2 if halves else tokens
    sums = [F32, BF16] if halves else [F32]
    sizes = sorted({span // 2, span - 2 * LANES, span - LANES, span})
    smem = pl.BlockSpec(memory_space=pltpu.SMEM)
    vmem = pl.BlockSpec(memory_space=pltpu.VMEM)
    hbm = pl.BlockSpec(memory_space=pl.ANY)
    two = lambda shape, kind: [pltpu.VMEM(shape, kind)] * 2
    return pl.pallas_call(
        functools.partial(attend_kernel, tokens, depth ** (-0.5), halves, sizes),
        in_specs=[smem, smem, vmem, hbm, hbm, hbm, hbm, vmem],
        out_specs=[hbm] + [vmem] * len(sums),
        out_shape=[
            jax.ShapeDtypeStruct((heads, depth, tokens), BF16),
            *[jax.ShapeDtypeStruct((span // tokens, width, share), kind) for kind in sums],
        ],
        scratch_shapes=[
            pltpu.VMEM((heads, depth, tokens), BF16),
            pltpu.VMEM((heads, tokens, vdim), BF16),
            pltpu.VMEM((heads, latw, nope), BF16),
            pltpu.VMEM((heads, latw, vdim), BF16),
            pltpu.VMEM((heads, depth, tokens), BF16),
            pltpu.VMEM((span, width), BF16),
            pltpu.VMEM((span, tokens), F32),
            pltpu.VMEM((span, width), F32),
            pltpu.VMEM((4, span, nope + vdim), BF16),
            two((span, tokens), F32),
            two((span, tokens), F32),
            two((span, tokens), BF16),
            two((span, tokens), BF16),
            two((span, nope + vdim), BF16),
            two((1, tokens), F32),
            two((1, tokens), F32),
            pltpu.SemaphoreType.DMA((4, heads)),
            pltpu.SemaphoreType.DMA((heads,)),
        ],
        compiler_params=pltpu.CompilerParams(vmem_limit_bytes=60 * 1024 * 1024),
        name="attend",
    )(count, side, starts, q, g, uk, uv, keys)


def places():
    me = lax.axis_index("seq")
    count = lax.axis_size("seq")
    head = lax.axis_index("head")
    ahead = [(lax.rem(me + r, count), head) for r in range(1, BACK + 1)]
    behind = [(lax.rem(me + count - r, count), head) for r in range(1, BACK + 1)]
    return head, ahead, behind, (me, 1 - head)


def meet(peers):
    barrier = pltpu.get_barrier_semaphore()
    for peer in peers:
        pl.semaphore_signal(barrier, inc=1, device_id=peer, device_id_type=pl.DeviceIdType.MESH)
    pl.semaphore_wait(barrier, len(peers))


def send(src, dst, sems, slot, peer):
    copy = pltpu.make_async_remote_copy(
        src_ref=src, dst_ref=dst, send_sem=sems.at[0, slot], recv_sem=sems.at[1, slot],
        device_id=peer, device_id_type=pl.DeviceIdType.MESH,
    )
    copy.start()
    return copy


def gather_kernel(own_ref, keys_ref, far_sems, near_sems):
    tokens = own_ref.shape[1]
    half = tokens // 2
    head, ahead, behind, sibling = places()
    meet(ahead + behind + [sibling])
    mine = pl.ds(pl.multiple_of(head * half, half), half)
    landing = [
        keys_ref.at[:, pl.ds(pl.multiple_of((BACK - r) * tokens + head * half, half), half)]
        for r in range(1, BACK + 1)
    ]
    far = [send(own_ref.at[:, mine], landing[r], far_sems, r, ahead[r]) for r in range(BACK)]
    keys_ref[:, BACK * tokens:] = own_ref[...]
    near = []
    for r in range(BACK):
        far[r].wait_recv()
        near.append(send(landing[r], landing[r], near_sems, r, sibling))
    for r in range(BACK):
        far[r].wait_send()
        near[r].wait()


def gather(own):
    width, tokens = own.shape
    return pl.pallas_call(
        gather_kernel,
        out_shape=jax.ShapeDtypeStruct((width, (BACK + 1) * tokens), own.dtype),
        in_specs=[pl.BlockSpec(memory_space=pltpu.VMEM)],
        out_specs=pl.BlockSpec(memory_space=pltpu.VMEM),
        scratch_shapes=[pltpu.SemaphoreType.DMA((2, BACK)), pltpu.SemaphoreType.DMA((2, BACK))],
        compiler_params=pltpu.CompilerParams(collective_id=0, has_side_effects=True),
        name="gather",
    )(own)


def combine_kernel(mine_ref, theirs_ref, out_ref, near_ref, part_ref, far_ref, near_sems, far_sems):
    _, ahead, behind, sibling = places()
    meet(ahead + behind + [sibling])
    near = [
        send(theirs_ref.at[r], near_ref.at[r], near_sems, r, sibling) for r in range(BACK + 1)
    ]
    far = []
    for r in range(BACK):
        near[r].wait_recv()
        part_ref[r] = (mine_ref[r] + near_ref[r].astype(F32)).astype(BF16)
        far.append(send(part_ref.at[r], far_ref.at[r], far_sems, r, behind[BACK - 1 - r]))
    near[BACK].wait_recv()
    out_ref[...] = mine_ref[BACK] + near_ref[BACK].astype(F32)
    for r in range(BACK):
        far[r].wait_recv()
        out_ref[...] += far_ref[r].astype(F32)
    for r in range(BACK + 1):
        near[r].wait_send()
    for r in range(BACK):
        far[r].wait_send()


def combine(mine, theirs):
    shape = mine.shape[1:]
    return pl.pallas_call(
        combine_kernel,
        out_shape=jax.ShapeDtypeStruct(shape, F32),
        in_specs=[pl.BlockSpec(memory_space=pltpu.VMEM)] * 2,
        out_specs=pl.BlockSpec(memory_space=pltpu.VMEM),
        scratch_shapes=[
            pltpu.VMEM((BACK + 1,) + shape, BF16),
            pltpu.VMEM((BACK,) + shape, BF16),
            pltpu.VMEM((BACK,) + shape, BF16),
            pltpu.SemaphoreType.DMA((2, BACK + 1)),
            pltpu.SemaphoreType.DMA((2, BACK)),
        ],
        compiler_params=pltpu.CompilerParams(collective_id=1, has_side_effects=True),
        name="combine",
    )(mine, theirs)


def shift(block, axis, distance):
    devices = range(lax.axis_size(axis))
    route = [(i - distance, i) for i in devices if i - distance in devices]
    return lax.ppermute(block, axis, route)


def shards(queries, grad_out, latent, w_uk, w_uv, doc_start):
    tokens, heads, depth = queries.shape
    span = (BACK + 1) * tokens
    own = latent.T
    halves = lax.axis_size("head") == 2
    if halves:
        keys = gather(own)
    else:
        received = [shift(own, "seq", level) for level in range(BACK, 0, -1)]
        keys = jnp.concatenate(received + [own], 1)
    starts = doc_start - (lax.axis_index("seq") - BACK) * tokens
    count = span // LANES - starts[:1] // LANES
    side = lax.axis_index("head").astype(jnp.int32)[None]
    grad_q, mine, *theirs = attend(
        count,
        side,
        starts[None, :],
        queries.transpose(1, 2, 0),
        grad_out.transpose(1, 0, 2),
        w_uk,
        w_uv,
        keys,
        halves,
    )
    grad_query = grad_q.transpose(2, 0, 1)
    if halves:
        return grad_query, combine(mine, theirs[0]).T
    back = [shift(mine[BACK - r].astype(BF16), "seq", -r) for r in range(1, BACK + 1)]
    total = mine[BACK]
    for piece in back:
        total = total + piece.astype(F32)
    return grad_query, lax.psum_scatter(total.T, "head", scatter_dimension=0, tiled=True)


def solution(mesh):
    placed = (
        P("seq", "head", None),
        P("seq", "head", None),
        P("seq", None),
        P("head", None, None),
        P("head", None, None),
        P("seq"),
    )
    return jax.shard_map(
        shards,
        mesh=mesh,
        in_specs=placed,
        out_specs=(P("seq", "head", None), P(("seq", "head"), None)),
        check_vma=False,
    )
```

time: 125 us -> 103 us (0.82); the launches traced: 127 us -> 104 us
  Pallas kernels: 120 us -> 93.7 us
  between operations: 0.66 us -> 3.27 us
    pallas_call x1, Pallas kernels: 55.3 us -> 41.5 us  [combine(): pl.pallas_call(combine_kernel, out_shape=jax.ShapeDtypeStruct(shape, F32)...]
    pallas_call x1, Pallas kernels: 46.7 us -> 34.5 us  [attend(): pl.pallas_call(functools.partial(attend_kernel, tokens, depth ** (-0.5),...]
where the time goes in v1:
time: 103 us; the launch traced here: 104 us
  Pallas kernels  93.7 us (91%)
  local copies, waits for them, and re-layouts  5.96 us (6%)
  between operations  3.27 us (3%)
    pallas_call x1, Pallas kernels, combine(): pl.pallas_call(combine_kernel, out_shape=jax.ShapeDtypeStruct(shape, F32)...  41.5 us
    pallas_call x1, Pallas kernels, attend(): pl.pallas_call(functools.partial(attend_kernel, tokens, depth ** (-0.5),...  34.5 us
    pallas_call x1, Pallas kernels, gather(): pl.pallas_call(gather_kernel, out_shape=jax.ShapeDtypeStruct((width, (BAC...  17.8 us
    unnamed x4, local copies, waits for them, and re-layouts  5.44 us

profile of v1, /device:TPU:0, one launch (start us, length us, event | category | flops | bytes accessed | tf_op | source)
XLA Modules:
  0.0 103.6 jit_solution(9112218322917736469)
XLA Ops:
  0.6 0.7 broadcast_subtract_fusion
  1.3 0.0 copy-start
  1.3 0.5 slice.3
  4.4 17.8 %gather.1.kt_ref = bf16[576,1024]{1,0:T(8,128)(2,1)} custom-call(bf16[576,256]{1,0:T(8,128)(2,1)} %bitcast.12), custom_call_target="tpu_custom_call" | custom-call | tf_op jit(solution)/shard_map/gather/pallas_call | solution.py:256
  22.2 3.7 %copy.10 = bf16[256,32,128]{2,0,1:T(8,128)(2,1)} copy(bf16[256,32,128]{2,1,0:T(8,128)(2,1)} %param.7) | data formatting | bytes 4194304 | tf_op args[1]
  26.0 0.0 copy-done
  26.0 34.5 %attend.1 = (bf16[32,192,256]{2,1,0:T(8,128)(2,1)}, f32[4,576,128]{2,1,0:T(8,128)}, bf16[4,576,128]{2,1,0:T(8,128)(2,1)}) custom-call(s32[1]{0:T(128)S(6)} %sub.20.count, s32[1]{0:T(128)} %bitcast.side, s32[1,256]{1,0:T(1,128)} %bitcast.13, bf16[32,192,256]{2,1,0:T(8,128)(2,1)} %bitcast.10, bf16[32,256,128]{2,1,0:T(8,128)(2,1)} %bitcast.9, ...), custom_call_target="tpu_custom_call" | custom-call | tf_op jit(solution)/shard_map/attend/pallas_call | solution.py:175
  60.4 41.5 %combine.1 = f32[576,128]{1,0:T(8,128)} custom-call(f32[4,576,128]{2,1,0:T(8,128)} %get-tuple-element.6.mine_ref, bf16[4,576,128]{2,1,0:T(8,128)(2,1)} %get-tuple-element.7.theirs_ref), custom_call_target="tpu_custom_call" | custom-call | tf_op jit(solution)/shard_map/combine/pallas_call | solution.py:291
  102.0 1.7 %copy.12 = f32[128,576]{0,1:T(8,128)} copy(f32[128,576]{0,1:T(8,128)} %bitcast.11) | data formatting | bytes 589824
Async XLA Ops:
  1.3 24.7 %copy-start = (s32[256]{0:T(256)}, s32[256]{0:T(256)S(1)}, u32[]{:S(2)}) copy-start(s32[256]{0:T(256)S(1)} %broadcast_subtract_fusion) | copy-start | bytes 3076
